TPU v7x, 32 devices: a whole 2x2x4 slice. The times are simulated.
32 devices in a mesh: dst: 8 (over z, core), src: 4 (over y, x).
Axes of the slice: x: 2, y: 2, z: 4, core: 2. Of those that a mesh axis runs over, the one named last changes fastest.
Arguments:
- features: bfloat16 [256, 3712], P(('dst', 'src')), may hold values from -6 to 6
- edge_source: int32 [8, 2048], P('dst', 'src'), may hold values from 0 to 255, as said below
- edge_target: int32 [8, 2048], P('dst', 'src'), may hold values from 0 to 255, as said below
- edge_valid: int32 [8, 2048], P('dst', 'src'), may hold values from 0 to 1, as said below
- edge_radial: bfloat16 [8, 2048, 128], P('dst', 'src'), may hold values from -6 to 6
- edge_bias: float32 [8, 8, 2048], P('dst', None, 'src'), may hold values from -10 to 330
- w_radial: bfloat16 [128, 128], replicated, may hold values from -0.5 to 0.5
- w_zero: bfloat16 [896, 896], replicated, may hold values from -0.1875 to 0.1875
- w_one_re: bfloat16 [768, 768], replicated, may hold values from -0.15625 to 0.15625
- w_one_im: bfloat16 [768, 768], replicated, may hold values from -0.15625 to 0.15625
- w_two_re: bfloat16 [640, 640], replicated, may hold values from -0.15625 to 0.15625
- w_two_im: bfloat16 [640, 640], replicated, may hold values from -0.15625 to 0.15625
- att_vector: float32 [128], replicated, may hold values from -3 to 3
- w_out: bfloat16 [7, 128, 128], replicated, may hold values from -0.5 to 0.5
Outputs:
- attended: bfloat16 [256, 3712], P(('dst', 'src'))
Inputs may be any that keep to these rules, and one draw needn't show every extreme that they name: `edge_source`: in row d, column block s (the tile of destination block d and source block s) every entry is an atom a with (a // 8) % 4 == s. `edge_target`: in row d every entry lies in [d * 8 * 4, (d + 1) * 8 * 4); every atom is the target of at least one valid slot. `edge_valid`: about five sixteenths of the slots are valid.
All inputs are finite; a program needn't handle non-finite values.
Results may differ from a plain program's by a relative error of at most 0.0093.
Values may be sent and summed in bfloat16 or wider, within the bound.
A program may use at most 128 MiB of HBM per device.

v0:
```python
import jax
import jax.numpy as jnp
import numpy as np
from jax import lax
from jax.sharding import PartitionSpec as P

HEADS = 8
NCOEF = 29
NEG = -1e30


def merged_2(part, axis, combine):
    gathered = jax.tree.map(lambda a: lax.all_gather(a, axis), part)

    def take(source):
        return jax.tree.map(lambda a: lax.dynamic_index_in_dim(a, source, 0, False), gathered)

    return lax.fori_loop(
        1, lax.axis_size(axis), lambda source, state: combine(state, take(source)), take(0)
    )


def product(left, right):
    return jnp.dot(left, right, preferred_element_type=jnp.float32)


def exact_product(left, right):
    return jnp.dot(left, right, precision=lax.Precision.HIGHEST, preferred_element_type=jnp.float32)


def spread_heads(weights, copies, channels):
    return jnp.tile(jnp.repeat(weights, channels // weights.shape[1], axis=1), (1, copies))


def degree_table():
    return np.array(list(range(7)) + list(range(1, 7)) * 2 + list(range(2, 7)) * 2, dtype=np.int32)


def edge_messages(rows, gain, w_zero, w_one_re, w_one_im, w_two_re, w_two_im, att_vector):
    channels = gain.shape[1]
    count = rows.shape[0]

    def part(low, high):
        return (
            rows[:, low * channels : high * channels].astype(jnp.float32)
            * jnp.tile(gain, (1, high - low))
        ).astype(jnp.bfloat16)

    zero = part(0, 7)
    up_one, uq_one = (part(7, 13), part(13, 19))
    up_two, uq_two = (part(19, 24), part(24, 29))
    out_zero = product(zero, w_zero)
    yp_one = product(up_one, w_one_re) - product(uq_one, w_one_im)
    yq_one = product(up_one, w_one_im) + product(uq_one, w_one_re)
    yp_two = product(up_two, w_two_re) - product(uq_two, w_two_im)
    yq_two = product(up_two, w_two_im) + product(uq_two, w_two_re)
    active = jax.nn.silu(out_zero[:, :channels]) * att_vector[None, :]
    logit = active.reshape(count, HEADS, channels // HEADS).sum(axis=2)
    values = jnp.concatenate([out_zero, yp_one, yq_one, yp_two, yq_two], axis=1)
    return (logit, values)


def shards(
    features,
    edge_source,
    edge_target,
    edge_valid,
    edge_radial,
    edge_bias,
    w_radial,
    w_zero,
    w_one_re,
    w_one_im,
    w_two_re,
    w_two_im,
    att_vector,
    w_out,
):
    channels = w_radial.shape[1]
    own_atoms = features.shape[0]
    block_atoms = own_atoms * lax.axis_size("src")
    gathered = lax.all_gather(features, "dst", axis=0, tiled=True)
    source = edge_source[0]
    target = edge_target[0]
    valid = edge_valid[0] > 0
    slots = source.shape[0]
    local_rows = source // block_atoms * own_atoms + source % own_atoms
    rows = jnp.take(gathered, local_rows, axis=0)
    gain = product(edge_radial[0], w_radial)
    logit, values = edge_messages(
        rows, gain, w_zero, w_one_re, w_one_im, w_two_re, w_two_im, att_vector
    )
    logit = logit + edge_bias[0].T
    local_target = target - lax.axis_index("dst") * block_atoms
    member = (
        lax.broadcasted_iota(jnp.int32, (block_atoms, slots), 0) == local_target[None, :]
    ) & valid[None, :]
    one_hot = member.astype(jnp.float32)
    local_top = jnp.max(jnp.where(member[:, :, None], logit[None, :, :], NEG), axis=1)
    edge_top = exact_product(one_hot.T, local_top)
    shifted = jnp.where(valid[:, None], logit - edge_top, 0.0)
    weights = jnp.where(valid[:, None], jnp.exp(shifted), 0.0)
    weighted = values * spread_heads(weights, NCOEF, channels)
    local_den = exact_product(one_hot, weights)
    local_num = exact_product(one_hot, weighted)

    def combine_states(first, second):
        top = jnp.maximum(first[0], second[0])
        scale_first = jnp.exp(first[0] - top)
        scale_second = jnp.exp(second[0] - top)
        den = first[1] * scale_first + second[1] * scale_second
        num = first[2] * spread_heads(scale_first, NCOEF, channels) + second[2] * spread_heads(
            scale_second, NCOEF, channels
        )
        return (top, den, num)

    merged_top, merged_den, merged_num = merged_2(
        (local_top, local_den, local_num), "src", combine_states
    )
    start = lax.axis_index("src") * own_atoms
    own_den = lax.dynamic_slice_in_dim(merged_den, start, own_atoms, 0)
    own_num = lax.dynamic_slice_in_dim(merged_num, start, own_atoms, 0)
    merged = (own_num / spread_heads(own_den, NCOEF, channels)).astype(jnp.bfloat16)
    selected = w_out[degree_table()]
    projected = jnp.einsum(
        "acx,cxy->acy",
        merged.reshape(own_atoms, NCOEF, channels),
        selected,
        preferred_element_type=jnp.float32,
    )
    return projected.astype(jnp.bfloat16).reshape(own_atoms, NCOEF * channels)


def solution(mesh):
    in_specs = (
        P(("dst", "src"), None),
        P("dst", "src"),
        P("dst", "src"),
        P("dst", "src"),
        P("dst", "src", None),
        P("dst", None, "src"),
        P(),
        P(),
        P(),
        P(),
        P(),
        P(),
        P(),
        P(),
    )
    out_specs = P(("dst", "src"), None)
    return jax.shard_map(shards, mesh=mesh, in_specs=in_specs, out_specs=out_specs, check_vma=False)
```

profile of v0, /device:TPU:0, one launch (start us, length us, event | category | flops | bytes accessed | tf_op | source)
XLA Modules:
  0.0 141.0 jit_solution(15630821081774154500)
XLA Ops:
  6.5 1.2 fusion.13
  7.8 0.7 copy-done.10
  8.5 0.2 tile.103
  8.8 1.7 %copy.53 = f32[512,896]{1,0:T(8,128)} copy(f32[512,896]{0,1:T(8,128)S(1)} %bitcast.111) | data formatting | bytes 3670016 | tf_op jit(solution)/shard_map/tile | solution.py:46
  10.5 16.4 %all_gather.21 = bf16[64,3712]{1,0:T(8,128)(2,1)S(1)} all-gather(bf16[8,3712]{1,0:T(8,128)(2,1)S(1)} %copy-done.16), channel_id=1, replica_groups=mesh['dst'=8,'src'=4] {'dst'}, dimensions={0}, use_global_device_ids=true | all-gather | bytes 534528 | tf_op jit(solution)/shard_map/all_gather | solution.py:82
  27.0 4.3 %gather_fusion.1 = bf16[512,3712]{1,0:T(8,128)(2,1)} fusion(bf16[64,3712]{1,0:T(8,128)(2,1)S(1)} %all_gather.21, s32[1024]{0:T(1024)S(1)} %pad_clamp_fusion), kind=kCustom, calls=%fused_computation.1 | custom fusion | bytes 7604224 | tf_op jit(solution)/shard_map/jit(_take)/gather | solution.py:88
  31.3 2.7 %broadcast_select_fusion = bf16[512,3712]{1,0:T(8,128)(2,1)S(1)} fusion(bf16[512,3712]{1,0:T(8,128)(2,1)} %gather_fusion.1, pred[512]{0:T(512)(128)(4,1)S(1)} %compare_and_fusion), kind=kLoop, calls=%fused_computation.13 | loop fusion | flops 1900544 | bytes 7602688 | tf_op jit(solution)/shard_map/jit(_take)/select_n | solution.py:88
  34.0 2.5 %constant_dynamic-update-slice_fusion = (f32[512,3712]{1,0:T(8,128)}, f32[512,896]{1,0:T(8,128)S(1)}) fusion(bf16[896,896]{1,0:T(8,128)(2,1)S(1)} %copy-done, f32[512,896]{1,0:T(8,128)S(1)} %copy-done.5, bf16[512,3712]{1,0:T(8,128)(2,1)S(1)} %broadcast_select_fusion), kind=kOutput, calls=%fused_computation.46 | convolution fusion | flops 823459840 | bytes 8028160 | tf_op jit(solution)/shard_map/dot_general | solution.py:24
  36.5 0.1 multiply_multiply_fusion
  36.6 0.1 copy.54
  36.9 0.2 select_reduce_fusion
  37.1 0.2 fusion.10
  37.3 0.2 copy-done.11
  37.5 1.4 tile.105
  38.8 1.9 %copy.57 = f32[512,768]{1,0:T(8,128)S(1)} copy(f32[512,768]{0,1:T(8,128)} %bitcast.114) | data formatting | bytes 3145728 | tf_op jit(solution)/shard_map/tile | solution.py:46
  40.7 3.6 %fusion.32 = f32[512,768]{1,0:T(8,128)} fusion(bf16[768,768]{1,0:T(8,128)(2,1)} %param.26, f32[512,768]{1,0:T(8,128)S(1)} %copy.57, bf16[512,3712]{1,0:T(8,128)(2,1)} %copy-done.3), kind=kOutput, calls=%fused_computation.80 | convolution fusion | flops 605159424 | bytes 5111808 | tf_op jit(solution)/shard_map/dot_general | solution.py:24
  44.4 3.1 %fusion.31 = f32[512,768]{1,0:T(8,128)} fusion(bf16[768,768]{1,0:T(8,128)(2,1)S(1)} %copy-done.9, f32[512,768]{1,0:T(8,128)S(1)} %copy.57, bf16[512,3712]{1,0:T(8,128)(2,1)} %copy-done.3), kind=kOutput, calls=%fused_computation.79 | convolution fusion | flops 605159424 | bytes 5111808 | tf_op jit(solution)/shard_map/dot_general | solution.py:24
  47.4 1.2 tile.107
  48.7 2.8 %copy.60 = f32[512,640]{1,0:T(8,128)} copy(f32[512,640]{0,1:T(8,128)} %bitcast.115) | data formatting | bytes 2621440 | tf_op jit(solution)/shard_map/tile | solution.py:46
  51.5 3.7 %fusion.30 = f32[512,640]{1,0:T(8,128)} fusion(bf16[640,640]{1,0:T(8,128)(2,1)} %param.28, f32[512,640]{1,0:T(8,128)} %copy.60, bf16[512,3712]{1,0:T(8,128)(2,1)} %copy-done.3), kind=kOutput, calls=%fused_computation.78 | convolution fusion | flops 420413440 | bytes 4096000 | tf_op jit(solution)/shard_map/dot_general | solution.py:24
  55.2 2.9 %fusion.29 = f32[512,640]{1,0:T(8,128)} fusion(bf16[640,640]{1,0:T(8,128)(2,1)S(1)} %copy-done.13, f32[512,640]{1,0:T(8,128)S(1)} %copy-done.1, bf16[512,3712]{1,0:T(8,128)(2,1)} %copy-done.3), kind=kOutput, calls=%fused_computation.77 | convolution fusion | flops 420413440 | bytes 4096000 | tf_op jit(solution)/shard_map/dot_general | solution.py:24
  58.1 4.0 %tile.110 = f32[512,29,128]{0,2,1:T(8,128)} broadcast(f32[512,128]{0,1:T(8,128)S(1)} %bitcast.117), dimensions={0,2} | broadcast | bytes 7864320 | tf_op jit(solution)/shard_map/tile | solution.py:32
  62.2 8.8 %copy.62 = f32[512,3712]{1,0:T(8,128)} copy(f32[512,3712]{0,1:T(8,128)} %bitcast.110) | data formatting | bytes 15204352 | tf_op jit(solution)/shard_map/tile | solution.py:32
  71.0 4.1 %subtract_dynamic-update-slice_fusion = f32[512,3712]{1,0:T(8,128)} fusion(f32[512,3712]{1,0:T(8,128)} %get-tuple-element.202, f32[512,768]{1,0:T(8,128)} %fusion.32, bf16[768,768]{1,0:T(8,128)(2,1)} %param.27, f32[512,768]{1,0:T(8,128)S(1)} %copy.57, bf16[512,3712]{1,0:T(8,128)(2,1)} %copy-done.3), kind=kOutput, calls=%fused_computation.16 | convolution fusion | flops 605552640 | bytes 6684672 | tf_op jit(solution)/shard_map/dot_general | solution.py:24
  75.2 3.5 %add_dynamic-update-slice_fusion = f32[512,3712]{1,0:T(8,128)} fusion(f32[512,3712]{1,0:T(8,128)} %subtract_dynamic-update-slice_fusion, f32[512,768]{1,0:T(8,128)S(1)} %copy-done.6, bf16[768,768]{1,0:T(8,128)(2,1)} %param.26, f32[512,768]{1,0:T(8,128)S(1)} %copy.57, bf16[512,3712]{1,0:T(8,128)(2,1)S(1)} %copy-done.4), kind=kOutput, calls=%fused_computation.15 | convolution fusion | flops 605552640 | bytes 6684672 | tf_op jit(solution)/shard_map/dot_general | solution.py:24
  78.7 1.9 %fusion.6 = f32[512,3712]{1,0:T(8,128)} fusion(f32[512,3712]{1,0:T(8,128)} %add_dynamic-update-slice_fusion, f32[512,640]{1,0:T(8,128)S(1)} %copy-done.8, bf16[640,640]{1,0:T(8,128)(2,1)S(1)} %copy-done.14, f32[512,640]{1,0:T(8,128)S(1)} %copy-done.2, bf16[512,3712]{1,0:T(8,128)(2,1)S(1)} %copy-done.4), kind=kOutput, calls=%fused_computation.22 | convolution fusion | flops 420741120 | bytes 5406720 | tf_op jit(solution)/shard_map/dot_general | solution.py:24
  80.6 1.9 %fusion.5 = f32[512,3712]{1,0:T(8,128)} fusion(f32[512,3712]{1,0:T(8,128)} %fusion.6, f32[512,640]{1,0:T(8,128)S(1)} %copy-done.7, bf16[640,640]{1,0:T(8,128)(2,1)S(1)} %copy-done.15, f32[512,640]{1,0:T(8,128)S(1)} %copy-done.2, bf16[512,3712]{1,0:T(8,128)(2,1)S(1)} %copy-done.4), kind=kOutput, calls=%fused_computation.20 | convolution fusion | flops 420741120 | bytes 5406720 | tf_op jit(solution)/shard_map/dot_general | solution.py:24
  82.6 7.2 %fusion.3 = f32[32,3712]{1,0:T(8,128)} fusion(f32[512,3712]{1,0:T(8,128)} %fusion.5, f32[512,3712]{1,0:T(8,128)S(1)} %bitcast.109, s32[512]{0:T(512)S(1)} %bitcast.121, pred[512]{0:T(512)(128)(4,1)S(1)} %compare_reduce_fusion), kind=kOutput, calls=%fused_computation.11 | convolution fusion | flops 731742208 | bytes 15682048 | tf_op jit(solution)/shard_map/dot_general | solution.py:28
  89.8 0.1 copy.55
  89.9 1.6 %gather_fusion = bf16[29,128,128]{2,1,0:T(8,128)(2,1)} fusion(bf16[7,128,128]{2,1,0:T(8,128)(2,1)S(1)} %copy-done.12, s32[1024]{0:T(1024)S(1)} %pad_clamp_fusion.1), kind=kCustom, calls=%fused_computation | custom fusion | bytes 1900660 | tf_op jit(solution)/shard_map/gather | solution.py:124
  91.5 8.2 %all-gather.3 = f32[4,32,8]{1,2,0:T(8,128)S(1)} all-gather(f32[1,32,8]{1,2,0:T(8,128)S(1)} %copy.55), channel_id=2, replica_groups=mesh['dst'=8,'src'=4] {'src'}, dimensions={0}, use_global_device_ids=true | all-gather | bytes 5120 | tf_op jit(solution)/shard_map/all_gather | solution.py:13
  99.7 0.1 convolution_bitcast_fusion
  99.8 8.4 %all-gather.4 = f32[4,32,8]{1,2,0:T(8,128)S(1)} all-gather(f32[1,32,8]{1,2,0:T(8,128)S(1)} %convolution_bitcast_fusion), channel_id=3, replica_groups=mesh['dst'=8,'src'=4] {'src'}, dimensions={0}, use_global_device_ids=true | all-gather | bytes 5120 | tf_op jit(solution)/shard_map/all_gather | solution.py:13
  108.2 16.4 %all-gather.7.cloned.1.call-done = f32[128,3712]{1,0:T(8,128)} async-done(((f32[32,3712]{1,0:T(8,128)}), f32[128,3712]{1,0:T(8,128)}) %all-gather.7.cloned.1.call-update) | async-done | bytes 1900560 | tf_op jit(solution)/shard_map/all_gather | solution.py:13
  124.7 1.1 slice.44
  125.7 5.9 %while.19 = (s32[]{:T(128)}, f32[32,8]{0,1:T(8,128)S(1)}, f32[32,8]{0,1:T(8,128)S(1)}, f32[32,3712]{1,0:T(8,128)S(1)}, f32[4,32,8]{1,2,0:T(8,128)S(1)}, /*index=...) while((s32[]{:T(128)}, f32[32,8]{0,1:T(8,128)S(1)}, ...), condition=%wide.region_3.4_spmd, body=%wide.region_2.3_spmd.sunk | while | flops 357893 | bytes 3467415 | solution.py:18
  125.8 0.1 copy.75
  125.9 0.1 copy.76
  126.0 1.7 %fusion.50 = f32[32,3712]{1,0:T(8,128)S(1)} fusion(f32[4,8,29,128]{3,2,1,0:T(8,128)S(1)} %bitcast.106, f32[32,3712]{1,0:T(8,128)S(1)} %get-tuple-element.268, f32[4,8,29,128]{3,2,1,0:T(8,128)S(1)} %bitcast.107, f32[4,32,3712]{2,1,0:T(8,128)} %get-tuple-element.281, s32[]{:T(128)S(6)} %select_n.137), kind=kLoop, calls=%fused_computation.3.clone.1 | loop fusion | flops 356352 | bytes 2375684 | tf_op jit(solution)/shard_map/while/body/eval_jaxpr/add | solution.py:112
  128.0 1.7 %fusion.50 = f32[32,3712]{1,0:T(8,128)S(1)} fusion(f32[4,8,29,128]{3,2,1,0:T(8,128)S(1)} %bitcast.106, f32[32,3712]{1,0:T(8,128)S(1)} %get-tuple-element.268, f32[4,8,29,128]{3,2,1,0:T(8,128)S(1)} %bitcast.107, f32[4,32,3712]{2,1,0:T(8,128)} %get-tuple-element.281, s32[]{:T(128)S(6)} %select_n.137), kind=kLoop, calls=%fused_computation.3.clone.1 | loop fusion | flops 356352 | bytes 2375684 | tf_op jit(solution)/shard_map/while/body/eval_jaxpr/add | solution.py:112
  129.7 0.1 copy.75
  129.9 0.1 copy.76
  130.0 1.7 %fusion.50 = f32[32,3712]{1,0:T(8,128)S(1)} fusion(f32[4,8,29,128]{3,2,1,0:T(8,128)S(1)} %bitcast.106, f32[32,3712]{1,0:T(8,128)S(1)} %get-tuple-element.268, f32[4,8,29,128]{3,2,1,0:T(8,128)S(1)} %bitcast.107, f32[4,32,3712]{2,1,0:T(8,128)} %get-tuple-element.281, s32[]{:T(128)S(6)} %select_n.137), kind=kLoop, calls=%fused_computation.3.clone.1 | loop fusion | flops 356352 | bytes 2375684 | tf_op jit(solution)/shard_map/while/body/eval_jaxpr/add | solution.py:112
  131.7 0.1 constant_dynamic-slice_fusion
  131.7 0.1 copy.63
  131.8 0.1 broadcast_in_dim.91
  131.9 0.1 tile.112
  132.0 2.2 %fusion.7 = bf16[8,3712]{1,0:T(8,128)(2,1)} fusion(bf16[29,128,128]{2,1,0:T(8,128)(2,1)} %gather_fusion, f32[32,3712]{1,0:T(8,128)S(1)} %get-tuple-element.182, s32[]{:T(128)S(6)} %select_n.99, f32[8,128]{1,0:T(8,128)S(1)} %tile.112), kind=kOutput, calls=%fused_computation.26 | convolution fusion | flops 7691264 | bytes 1132548 | tf_op jit(solution)/shard_map/acx,cxy->acy/dot_general | solution.py:125
  (80 shorter events, 0.8 us)
Async XLA Ops:
  6.5 27.4 %copy-start = (bf16[896,896]{1,0:T(8,128)(2,1)S(1)}, bf16[896,896]{1,0:T(8,128)(2,1)}, u32[]{:S(2)}) copy-start(bf16[896,896]{1,0:T(8,128)(2,1)} %param.25) | copy-start | bytes 4816900
  6.5 118.1 %all-gather.7.cloned.1.call-start = ((), (), s32[]{:S(2)}) async-start(), calls=%async_computation | async-start | bytes 2375680 | tf_op jit(solution)/shard_map/all_gather | solution.py:13
  7.8 0.7 copy-start.10
  8.7 1.7 %copy-start.16 = (bf16[8,3712]{1,0:T(8,128)(2,1)S(1)}, bf16[8,3712]{1,0:T(8,128)(2,1)}, u32[]{:S(2)}) copy-start(bf16[8,3712]{1,0:T(8,128)(2,1)} %param.18) | copy-start | bytes 178180
  8.8 18.1 %copy-start.18 = (s32[1,512]{1,0:T(1,128)S(1)}, s32[1,512]{1,0:T(1,128)}, u32[]{:S(2)}) copy-start(s32[1,512]{1,0:T(1,128)} %param.19) | copy-start | bytes 6148
  31.3 2.7 %copy-start.5 = (f32[512,896]{1,0:T(8,128)S(1)}, f32[512,896]{1,0:T(8,128)}, u32[]{:S(2)}) copy-start(f32[512,896]{1,0:T(8,128)} %copy.53) | copy-start | bytes 5505028
  34.0 2.6 %copy-start.3 = (bf16[512,3712]{1,0:T(8,128)(2,1)}, bf16[512,3712]{1,0:T(8,128)(2,1)S(1)}, u32[]{:S(2)}) copy-start(bf16[512,3712]{1,0:T(8,128)(2,1)S(1)} %broadcast_select_fusion) | copy-start | bytes 11403268
  34.0 2.6 %copy-start.21 = (f32[128]{0:T(128)S(1)}, f32[128]{0:T(128)}, u32[]{:S(2)}) copy-start(f32[128]{0:T(128)} %param.30) | copy-start | bytes 1540
  34.0 2.8 %copy-start.19 = (s32[1,512]{1,0:T(1,128)S(1)}, s32[1,512]{1,0:T(1,128)}, u32[]{:S(2)}) copy-start(s32[1,512]{1,0:T(1,128)} %param.21) | copy-start | bytes 6148
  34.0 2.8 %copy-start.17 = (f32[1,8,512]{2,1,0:T(8,128)S(1)}, f32[1,8,512]{2,1,0:T(8,128)}, u32[]{:S(2)}) copy-start(f32[1,8,512]{2,1,0:T(8,128)} %param.23) | copy-start | bytes 49156
  34.0 2.9 %copy-start.20 = (s32[1,512]{1,0:T(1,128)S(1)}, s32[1,512]{1,0:T(1,128)}, u32[]{:S(2)}) copy-start(s32[1,512]{1,0:T(1,128)} %param.20) | copy-start | bytes 6148
  36.5 1.0 copy-start.11
  40.7 3.7 %copy-start.9 = (bf16[768,768]{1,0:T(8,128)(2,1)S(1)}, bf16[768,768]{1,0:T(8,128)(2,1)}, u32[]{:S(2)}) copy-start(bf16[768,768]{1,0:T(8,128)(2,1)} %param.27) | copy-start | bytes 3538948
  51.4 3.7 %copy-start.1 = (f32[512,640]{1,0:T(8,128)S(1)}, f32[512,640]{1,0:T(8,128)}, u32[]{:S(2)}) copy-start(f32[512,640]{1,0:T(8,128)} %copy.60) | copy-start | bytes 3932164
  51.4 3.7 %copy-start.13 = (bf16[640,640]{1,0:T(8,128)(2,1)S(1)}, bf16[640,640]{1,0:T(8,128)(2,1)}, u32[]{:S(2)}) copy-start(bf16[640,640]{1,0:T(8,128)(2,1)} %param.29) | copy-start | bytes 2457604
  71.0 4.2 %copy-start.4 = (bf16[512,3712]{1,0:T(8,128)(2,1)S(1)}, bf16[512,3712]{1,0:T(8,128)(2,1)}, u32[]{:S(2)}) copy-start(bf16[512,3712]{1,0:T(8,128)(2,1)} %copy-done.3) | copy-start | bytes 11403268
  71.0 4.2 %copy-start.6 = (f32[512,768]{1,0:T(8,128)S(1)}, f32[512,768]{1,0:T(8,128)}, u32[]{:S(2)}) copy-start(f32[512,768]{1,0:T(8,128)} %fusion.31) | copy-start | bytes 4718596
  71.0 7.7 %copy-start.8 = (f32[512,640]{1,0:T(8,128)S(1)}, f32[512,640]{1,0:T(8,128)}, u32[]{:S(2)}) copy-start(f32[512,640]{1,0:T(8,128)} %fusion.30) | copy-start | bytes 3932164
  75.1 3.5 %copy-start.2 = (f32[512,640]{1,0:T(8,128)S(1)}, f32[512,640]{1,0:T(8,128)}, u32[]{:S(2)}) copy-start(f32[512,640]{1,0:T(8,128)} %copy.60) | copy-start | bytes 3932164
  75.2 3.5 %copy-start.14 = (bf16[640,640]{1,0:T(8,128)(2,1)S(1)}, bf16[640,640]{1,0:T(8,128)(2,1)}, u32[]{:S(2)}) copy-start(bf16[640,640]{1,0:T(8,128)(2,1)} %param.29) | copy-start | bytes 2457604
  75.2 5.4 %copy-start.15 = (bf16[640,640]{1,0:T(8,128)(2,1)S(1)}, bf16[640,640]{1,0:T(8,128)(2,1)}, u32[]{:S(2)}) copy-start(bf16[640,640]{1,0:T(8,128)(2,1)} %param.28) | copy-start | bytes 2457604
  75.2 7.4 %slice-start = ((s8[7602176]{0:T(1024)(128)(4,1)}), s8[4194304]{0:T(1024)(128)(4,1)S(1)}, s32[]{:S(2)}) async-start(s8[7602176]{0:T(1024)(128)(4,1)} %bitcast.108), calls=%async_computation.1 | async-start | bytes 8388608
  78.7 1.9 %copy-start.7 = (f32[512,640]{1,0:T(8,128)S(1)}, f32[512,640]{1,0:T(8,128)}, u32[]{:S(2)}) copy-start(f32[512,640]{1,0:T(8,128)} %fusion.29) | copy-start | bytes 3932164
  78.7 3.8 %slice-start.1 = ((s8[7602176]{0:T(1024)(128)(4,1)}), s8[3407872]{0:T(1024)(128)(4,1)S(1)}, s32[]{:S(2)}) async-start(s8[7602176]{0:T(1024)(128)(4,1)} %bitcast.108), calls=%async_computation.2 | async-start | bytes 6815744
  82.5 7.3 %copy-start.22 = (s32[29]{0:T(128)S(1)}, s32[29]{0:T(128)}, u32[]{:S(2)}) copy-start(s32[29]{0:T(128)} %constant.134) | copy-start | bytes 352
  82.5 7.3 %copy-start.12 = (bf16[7,128,128]{2,1,0:T(8,128)(2,1)S(1)}, bf16[7,128,128]{2,1,0:T(8,128)(2,1)}, u32[]{:S(2)}) copy-start(bf16[7,128,128]{2,1,0:T(8,128)(2,1)} %param.31) | copy-start | bytes 688132
Sparse Core Ops, SparseCore 0:
  89.9 34.7 all-gather.6
where the time goes:
time: 142 us; the launch traced here: 141 us
  matrix products  38.3 us (27%)
  blocking collectives  33 us (23%)
  local copies, waits for them, and re-layouts  31.2 us (22%)
  waiting for transfers between devices  16.5 us (12%)
  between operations  13.7 us (10%)
  other arithmetic  8.12 us (6%)
    dot_general x10, matrix products, product(): return jnp.dot(left, right, preferred_element_type=jnp.float32)  28.6 us
    all_gather x2, blocking collectives, merged_2(): gathered = jax.tree.map(lambda a: lax.all_gather(a, axis), part)  16.6 us
    all_gather x1, waiting for transfers between devices, merged_2(): gathered = jax.tree.map(lambda a: lax.all_gather(a, axis), part)  16.4 us
    all_gather x1, blocking collectives, shards(): gathered = lax.all_gather(features, 'dst', axis=0, tiled=True)  16.4 us
    another operation x15, local copies, waits for them, and re-layouts, spread_heads(): jnp.tile(jnp.repeat(weights, channels // weights.shape[1], axis=1), (1, c...  13.6 us
    another operation x6, local copies, waits for them, and re-layouts, part(): jnp.tile(gain, (1, high - low))  9.16 us
    dot_general x3, matrix products, exact_product(): jnp.dot(left, right, precision=lax.Precision.HIGHEST, preferred_element_t...  7.55 us
    add x3, other arithmetic, combine_states(): first[2] * spread_heads(scale_first, NCOEF, channels)  5.02 us
  transfers between devices with their start and end apart: 1, of which 1 were waited for; matrix products, arithmetic and copies ran while one was open for 1% of the time, Pallas kernels for 0%

commit v1 on v0

--- a/solution.py
+++ b/solution.py
@@ -1,3 +1,4 @@
+import functools
 import jax
 import jax.numpy as jnp
 import numpy as np
@@ -7,6 +8,36 @@
 HEADS = 8
 NCOEF = 29
 NEG = -1e30
+
+
+def lead_edges_over_axis(u, dimension_no):
+    everything = list(u.shape[1:])
+    everything[dimension_no] *= u.shape[0]
+    return jnp.moveaxis(u, 0, dimension_no).reshape(everything)
+
+
+def clear_the_seats_all(s0, device_axis):
+    small = lax.psum(1, device_axis)
+    reached = lax.axis_index(device_axis)
+    current_arr, passed = (small, reached)
+    e_next, m_next = (s0[None], 1)
+    while m_next < current_arr:
+        f_now = tuple(((tick, tick ^ m_next) for tick in range(current_arr)))
+        block_next = lax.ppermute(e_next, device_axis, f_now)
+        t_next = passed & m_next == 0
+        mixed_arr = jnp.where(t_next, e_next, block_next)
+        response = jnp.where(t_next, block_next, e_next)
+        e_next = jnp.concatenate([mixed_arr, response])
+        m_next *= 2
+    return e_next
+
+
+def targets_use(xs, vec, dim_k):
+    z = clear_the_seats_all(xs, vec)
+    return lead_edges_over_axis(z, dim_k)
+
+
+rest_roots = functools.partial(targets_use, vec="dst", dim_k=0)
 
 
 def merged_2(part, axis, combine):
@@ -79,7 +110,7 @@
     channels = w_radial.shape[1]
     own_atoms = features.shape[0]
     block_atoms = own_atoms * lax.axis_size("src")
-    gathered = lax.all_gather(features, "dst", axis=0, tiled=True)
+    gathered = rest_roots(features)
     source = edge_source[0]
     target = edge_target[0]
     valid = edge_valid[0] > 0

time: 142 us -> 138 us (0.972)
  blocking collectives: 33 us -> 16.4 us
  other arithmetic: 8.12 us -> 14.5 us
  waiting for transfers between devices: 16.5 us -> 22.7 us
  starting transfers between devices: 0.01 us -> 6 us
  matrix products: 38.3 us -> 34.8 us
  local copies, waits for them, and re-layouts: 31.2 us -> 29.1 us
    all_gather x1 -> x0, blocking collectives: 16.4 us -> none  [shards(): gathered = lax.all_gather(features, 'dst', axis=0, tiled=True)]
    ppermute x0 -> x3, waiting for transfers between devices: none -> 6.07 us  [clear_the_seats_all(): block_next = lax.ppermute(e_next, device_axis, f_now)]
    ppermute x0 -> x3, starting transfers between devices: none -> 5.99 us  [clear_the_seats_all(): block_next = lax.ppermute(e_next, device_axis, f_now)]
    dot_general x10, matrix products: 28.6 us -> 25 us  [product(): return jnp.dot(left, right, preferred_element_type=jnp.float32)]
    another operation x6, local copies, waits for them, and re-layouts: 9.16 us -> 7.27 us  [part(): jnp.tile(gain, (1, high - low))]
    select_n x0 -> x3, other arithmetic: none -> 1.87 us  [clear_the_seats_all(): mixed_arr = jnp.where(t_next, e_next, block_next)]
  transfers between devices with their start and end apart: 1 -> 4, of which waited for: 1 -> 3; matrix products, arithmetic and copies ran while one was open for 1% -> 10% of each run, Pallas kernels for 0% -> 0%
where the time goes in v1:
time: 138 us; the launch traced here: 137 us
  matrix products  34.8 us (25%)
  local copies, waits for them, and re-layouts  29.1 us (21%)
  waiting for transfers between devices  22.7 us (16%)
  blocking collectives  16.4 us (12%)
  other arithmetic  14.5 us (11%)
  between operations  13.7 us (10%)
  starting transfers between devices  6 us (4%)
    dot_general x10, matrix products, product(): return jnp.dot(left, right, preferred_element_type=jnp.float32)  25 us
    all_gather x1, waiting for transfers between devices, merged_2(): gathered = jax.tree.map(lambda a: lax.all_gather(a, axis), part)  16.6 us
    all_gather x2, blocking collectives, merged_2(): gathered = jax.tree.map(lambda a: lax.all_gather(a, axis), part)  16.4 us
    another operation x15, local copies, waits for them, and re-layouts, spread_heads(): jnp.tile(jnp.repeat(weights, channels // weights.shape[1], axis=1), (1, c...  13.5 us
    dot_general x3, matrix products, exact_product(): jnp.dot(left, right, precision=lax.Precision.HIGHEST, preferred_element_t...  7.58 us
    another operation x6, local copies, waits for them, and re-layouts, part(): jnp.tile(gain, (1, high - low))  7.27 us
    ppermute x3, waiting for transfers between devices, clear_the_seats_all(): block_next = lax.ppermute(e_next, device_axis, f_now)  6.07 us
    ppermute x3, starting transfers between devices, clear_the_seats_all(): block_next = lax.ppermute(e_next, device_axis, f_now)  5.99 us
  transfers between devices with their start and end apart: 4, of which 3 were waited for; matrix products, arithmetic and copies ran while one was open for 10% of the time, Pallas kernels for 0%

profile of v1, /device:TPU:0, one launch (start us, length us, event | category | flops | bytes accessed | tf_op | source)
XLA Modules:
  0.0 137.4 jit_solution(14938162441934703827)
XLA Ops:
  6.5 0.5 collective-permute-start
  7.0 0.7 compare_select_fusion
  7.7 1.8 %fusion.13 = f32[512,128]{0,1:T(8,128)} fusion(bf16[128,128]{1,0:T(8,128)(2,1)} %param.24, bf16[1,512,128]{2,1,0:T(8,128)(2,1)} %param.22), kind=kOutput, calls=%fused_computation.41 | convolution fusion | flops 16777216 | bytes 425984 | tf_op jit(solution)/shard_map/dot_general | solution.py:55
  9.6 0.7 broadcast_subtract_fusion
  10.3 0.8 broadcast_select_fusion.6
  11.1 2.7 %collective-permute-start.1 = (bf16[2,8,3712]{2,1,0:T(8,128)(2,1)S(1)}, bf16[2,8,3712]{2,1,0:T(8,128)(2,1)S(1)}, u32[]{:S(2)}, u32[]{:S(2)}) collective-permute-start(bf16[2,8,3712]{2,1,0:T(8,128)(2,1)S(1)} %pad_maximum_fusion.1), channel_id=1, source_target_pairs={{0,8},{4,12},{8,0},{12,4},{16,24},{20,28},{24,16},{28,20},{1,9},{5... | collective-permute-start | bytes 356360 | tf_op jit(solution)/shard_map/ppermute | solution.py:26
  13.9 0.7 compare_and_fusion
  14.6 0.7 compare_reduce_fusion
  15.3 2.4 %collective-permute-done.1 = bf16[2,8,3712]{2,1,0:T(8,128)(2,1)S(1)} collective-permute-done((bf16[2,8,3712]{2,1,0:T(8,128)(2,1)S(1)}, bf16[2,8,3712]{2,1,0:T(8,128)(2,1)S(1)}, u32[]{:S(2)}, u32[]{:S(2)}) %collective-permute-start.1) | collective-permute-done | bytes 118816 | tf_op jit(solution)/shard_map/ppermute | solution.py:26
  17.7 0.8 pad_maximum_fusion
  18.5 2.8 %collective-permute-start.2 = (bf16[4,8,3712]{2,1,0:T(8,128)(2,1)}, bf16[4,8,3712]{2,1,0:T(8,128)(2,1)}, u32[]{:S(2)}, u32[]{:S(2)}) collective-permute-start(bf16[4,8,3712]{2,1,0:T(8,128)(2,1)} %pad_maximum_fusion), channel_id=1, source_target_pairs={{0,16},{4,20},{8,24},{12,28},{16,0},{20,4},{24,8},{28,12},{1,17},{... | collective-permute-start | bytes 712712 | tf_op jit(solution)/shard_map/ppermute | solution.py:26
  21.3 1.2 tile.103
  22.4 1.7 %copy.53 = f32[512,896]{1,0:T(8,128)} copy(f32[512,896]{0,1:T(8,128)S(1)} %bitcast.116) | data formatting | bytes 3670016 | tf_op jit(solution)/shard_map/tile | solution.py:77
  24.2 1.1 tile.105
  25.3 1.6 %copy.57 = f32[512,768]{1,0:T(8,128)} copy(f32[512,768]{0,1:T(8,128)S(1)} %bitcast.119) | data formatting | bytes 3145728 | tf_op jit(solution)/shard_map/tile | solution.py:77
  26.9 0.2 tile.107
  27.1 1.5 %copy.60 = f32[512,640]{1,0:T(8,128)} copy(f32[512,640]{0,1:T(8,128)S(1)} %bitcast.120) | data formatting | bytes 2621440 | tf_op jit(solution)/shard_map/tile | solution.py:77
  28.6 3.7 %collective-permute-done.2 = bf16[4,8,3712]{2,1,0:T(8,128)(2,1)} collective-permute-done((bf16[4,8,3712]{2,1,0:T(8,128)(2,1)}, bf16[4,8,3712]{2,1,0:T(8,128)(2,1)}, u32[]{:S(2)}, u32[]{:S(2)}) %collective-permute-start.2) | collective-permute-done | bytes 237600 | tf_op jit(solution)/shard_map/ppermute | solution.py:26
  32.3 1.0 broadcast_select_fusion.2
  33.4 4.3 %gather_fusion.1 = bf16[512,3712]{1,0:T(8,128)(2,1)} fusion(bf16[64,3712]{1,0:T(8,128)(2,1)S(1)} %maximum_bitcast_fusion, s32[1024]{0:T(1024)S(1)} %pad_clamp_fusion), kind=kCustom, calls=%fused_computation.1 | custom fusion | bytes 7604224 | tf_op jit(solution)/shard_map/jit(_take)/gather | solution.py:119
  37.7 2.7 %broadcast_select_fusion = bf16[512,3712]{1,0:T(8,128)(2,1)S(1)} fusion(bf16[512,3712]{1,0:T(8,128)(2,1)} %gather_fusion.1, pred[512]{0:T(512)(128)(4,1)S(1)} %compare_and_fusion), kind=kLoop, calls=%fused_computation.13 | loop fusion | flops 1900544 | bytes 7602688 | tf_op jit(solution)/shard_map/jit(_take)/select_n | solution.py:119
  40.4 2.5 %constant_dynamic-update-slice_fusion = (f32[512,3712]{1,0:T(8,128)}, f32[512,896]{1,0:T(8,128)S(1)}) fusion(bf16[896,896]{1,0:T(8,128)(2,1)S(1)} %copy-done, f32[512,896]{1,0:T(8,128)S(1)} %copy-done.7, bf16[512,3712]{1,0:T(8,128)(2,1)S(1)} %broadcast_select_fusion), kind=kOutput, calls=%fused_computation.55 | convolution fusion | flops 823459840 | bytes 8028160 | tf_op jit(solution)/shard_map/dot_general | solution.py:55
  43.0 0.8 copy.54
  43.8 1.0 bitcast_reduce_fusion
  44.8 0.2 select_reduce_fusion
  45.0 0.2 fusion.10
  45.2 3.7 %fusion.32 = f32[512,768]{1,0:T(8,128)} fusion(bf16[768,768]{1,0:T(8,128)(2,1)} %param.26, f32[512,768]{1,0:T(8,128)S(1)} %copy-done.1, bf16[512,3712]{1,0:T(8,128)(2,1)} %copy-done.4), kind=kOutput, calls=%fused_computation.89 | convolution fusion | flops 605159424 | bytes 5111808 | tf_op jit(solution)/shard_map/dot_general | solution.py:55
  48.9 1.9 %fusion.31 = f32[512,768]{1,0:T(8,128)} fusion(bf16[768,768]{1,0:T(8,128)(2,1)S(1)} %copy-done.11, f32[512,768]{1,0:T(8,128)S(1)} %copy-done.1, bf16[512,3712]{1,0:T(8,128)(2,1)S(1)} %copy-done.5), kind=kOutput, calls=%fused_computation.88 | convolution fusion | flops 605159424 | bytes 5111808 | tf_op jit(solution)/shard_map/dot_general | solution.py:55
  50.9 1.8 %fusion.30 = f32[512,640]{1,0:T(8,128)} fusion(bf16[640,640]{1,0:T(8,128)(2,1)S(1)} %copy-done.16, f32[512,640]{1,0:T(8,128)S(1)} %copy-done.2, bf16[512,3712]{1,0:T(8,128)(2,1)S(1)} %copy-done.5), kind=kOutput, calls=%fused_computation.87 | convolution fusion | flops 420413440 | bytes 4096000 | tf_op jit(solution)/shard_map/dot_general | solution.py:55
  52.8 1.8 %fusion.29 = f32[512,640]{1,0:T(8,128)} fusion(bf16[640,640]{1,0:T(8,128)(2,1)S(1)} %copy-done.14, f32[512,640]{1,0:T(8,128)S(1)} %copy-done.2, bf16[512,3712]{1,0:T(8,128)(2,1)S(1)} %copy-done.5), kind=kOutput, calls=%fused_computation.86 | convolution fusion | flops 420413440 | bytes 4096000 | tf_op jit(solution)/shard_map/dot_general | solution.py:55
  54.6 4.0 %tile.110 = f32[512,29,128]{0,2,1:T(8,128)} broadcast(f32[512,128]{0,1:T(8,128)S(1)} %bitcast.122), dimensions={0,2} | broadcast | bytes 7864320 | tf_op jit(solution)/shard_map/tile | solution.py:63
  58.6 8.8 %copy.62 = f32[512,3712]{1,0:T(8,128)} copy(f32[512,3712]{0,1:T(8,128)} %bitcast.115) | data formatting | bytes 15204352 | tf_op jit(solution)/shard_map/tile | solution.py:63
  67.4 4.1 %subtract_dynamic-update-slice_fusion = f32[512,3712]{1,0:T(8,128)} fusion(f32[512,3712]{1,0:T(8,128)} %get-tuple-element.208, f32[512,768]{1,0:T(8,128)} %fusion.32, bf16[768,768]{1,0:T(8,128)(2,1)} %param.27, f32[512,768]{1,0:T(8,128)S(1)} %copy-done.1, bf16[512,3712]{1,0:T(8,128)(2,1)} %copy-done.4), kind=kOutput, calls=%fused_computation.16 | convolution fusion | flops 605552640 | bytes 6684672 | tf_op jit(solution)/shard_map/dot_general | solution.py:55
  71.6 3.4 %add_dynamic-update-slice_fusion = f32[512,3712]{1,0:T(8,128)} fusion(f32[512,3712]{1,0:T(8,128)} %subtract_dynamic-update-slice_fusion, f32[512,768]{1,0:T(8,128)S(1)} %copy-done.8, bf16[768,768]{1,0:T(8,128)(2,1)} %param.26, f32[512,768]{1,0:T(8,128)S(1)} %copy-done.1, bf16[512,3712]{1,0:T(8,128)(2,1)S(1)} %copy-done.6), kind=kOutput, calls=%fused_computation.15 | convolution fusion | flops 605552640 | bytes 6684672 | tf_op jit(solution)/shard_map/dot_general | solution.py:55
  75.0 1.9 %fusion.6 = f32[512,3712]{1,0:T(8,128)} fusion(f32[512,3712]{1,0:T(8,128)} %add_dynamic-update-slice_fusion, f32[512,640]{1,0:T(8,128)S(1)} %copy-done.10, bf16[640,640]{1,0:T(8,128)(2,1)S(1)} %copy-done.15, f32[512,640]{1,0:T(8,128)S(1)} %copy-done.3, bf16[512,3712]{1,0:T(8,128)(2,1)S(1)} %copy-done.6), kind=kOutput, calls=%fused_computation.22 | convolution fusion | flops 420741120 | bytes 5406720 | tf_op jit(solution)/shard_map/dot_general | solution.py:55
  77.0 1.9 %fusion.5 = f32[512,3712]{1,0:T(8,128)} fusion(f32[512,3712]{1,0:T(8,128)} %fusion.6, f32[512,640]{1,0:T(8,128)S(1)} %copy-done.9, bf16[640,640]{1,0:T(8,128)(2,1)S(1)} %copy-done.17, f32[512,640]{1,0:T(8,128)S(1)} %copy-done.3, bf16[512,3712]{1,0:T(8,128)(2,1)S(1)} %copy-done.6), kind=kOutput, calls=%fused_computation.20 | convolution fusion | flops 420741120 | bytes 5406720 | tf_op jit(solution)/shard_map/dot_general | solution.py:55
  78.9 7.3 %fusion.3 = f32[32,3712]{1,0:T(8,128)} fusion(f32[512,3712]{1,0:T(8,128)} %fusion.5, f32[512,3712]{1,0:T(8,128)S(1)} %bitcast.114, s32[512]{0:T(512)S(1)} %bitcast.127, pred[512]{0:T(512)(128)(4,1)S(1)} %compare_reduce_fusion), kind=kOutput, calls=%fused_computation.11 | convolution fusion | flops 731742208 | bytes 15682048 | tf_op jit(solution)/shard_map/dot_general | solution.py:59
  86.2 1.6 %gather_fusion = bf16[29,128,128]{2,1,0:T(8,128)(2,1)} fusion(bf16[7,128,128]{2,1,0:T(8,128)(2,1)S(1)} %copy-done.13, s32[1024]{0:T(1024)S(1)} %pad_clamp_fusion.1), kind=kCustom, calls=%fused_computation | custom fusion | bytes 1900660 | tf_op jit(solution)/shard_map/gather | solution.py:155
  87.9 8.1 %all-gather.3 = f32[4,32,8]{1,2,0:T(8,128)S(1)} all-gather(f32[1,32,8]{1,2,0:T(8,128)S(1)} %copy.55), channel_id=2, replica_groups=mesh['dst'=8,'src'=4] {'src'}, dimensions={0}, use_global_device_ids=true | all-gather | bytes 5120 | tf_op jit(solution)/shard_map/all_gather | solution.py:44
  95.9 0.1 convolution_bitcast_fusion
  96.1 8.4 %all-gather.4 = f32[4,32,8]{1,2,0:T(8,128)S(1)} all-gather(f32[1,32,8]{1,2,0:T(8,128)S(1)} %convolution_bitcast_fusion), channel_id=3, replica_groups=mesh['dst'=8,'src'=4] {'src'}, dimensions={0}, use_global_device_ids=true | all-gather | bytes 5120 | tf_op jit(solution)/shard_map/all_gather | solution.py:44
  104.4 16.6 %all-gather.7.cloned.1.call-done = f32[128,3712]{1,0:T(8,128)} async-done(((f32[32,3712]{1,0:T(8,128)}), f32[128,3712]{1,0:T(8,128)}) %all-gather.7.cloned.1.call-update) | async-done | bytes 1900560 | tf_op jit(solution)/shard_map/all_gather | solution.py:44
  121.0 1.1 slice.44
  122.1 5.9 %while.19 = (s32[]{:T(128)}, f32[32,8]{0,1:T(8,128)S(1)}, f32[32,8]{0,1:T(8,128)S(1)}, f32[32,3712]{1,0:T(8,128)S(1)}, f32[4,32,8]{1,2,0:T(8,128)S(1)}, /*index=...) while((s32[]{:T(128)}, f32[32,8]{0,1:T(8,128)S(1)}, ...), condition=%wide.region_3.4_spmd, body=%wide.region_2.3_spmd.sunk | while | flops 357893 | bytes 3467415 | solution.py:49
  122.4 1.7 %fusion.50 = f32[32,3712]{1,0:T(8,128)S(1)} fusion(f32[4,8,29,128]{3,2,1,0:T(8,128)S(1)} %bitcast.111, f32[32,3712]{1,0:T(8,128)S(1)} %get-tuple-element.274, f32[4,8,29,128]{3,2,1,0:T(8,128)S(1)} %bitcast.112, f32[4,32,3712]{2,1,0:T(8,128)} %get-tuple-element.287, s32[]{:T(128)S(6)} %select_n.194), kind=kLoop, calls=%fused_computation.3.clone.1 | loop fusion | flops 356352 | bytes 2375684 | tf_op jit(solution)/shard_map/while/body/eval_jaxpr/add | solution.py:143
  124.4 1.7 %fusion.50 = f32[32,3712]{1,0:T(8,128)S(1)} fusion(f32[4,8,29,128]{3,2,1,0:T(8,128)S(1)} %bitcast.111, f32[32,3712]{1,0:T(8,128)S(1)} %get-tuple-element.274, f32[4,8,29,128]{3,2,1,0:T(8,128)S(1)} %bitcast.112, f32[4,32,3712]{2,1,0:T(8,128)} %get-tuple-element.287, s32[]{:T(128)S(6)} %select_n.194), kind=kLoop, calls=%fused_computation.3.clone.1 | loop fusion | flops 356352 | bytes 2375684 | tf_op jit(solution)/shard_map/while/body/eval_jaxpr/add | solution.py:143
  126.4 1.7 %fusion.50 = f32[32,3712]{1,0:T(8,128)S(1)} fusion(f32[4,8,29,128]{3,2,1,0:T(8,128)S(1)} %bitcast.111, f32[32,3712]{1,0:T(8,128)S(1)} %get-tuple-element.274, f32[4,8,29,128]{3,2,1,0:T(8,128)S(1)} %bitcast.112, f32[4,32,3712]{2,1,0:T(8,128)} %get-tuple-element.287, s32[]{:T(128)S(6)} %select_n.194), kind=kLoop, calls=%fused_computation.3.clone.1 | loop fusion | flops 356352 | bytes 2375684 | tf_op jit(solution)/shard_map/while/body/eval_jaxpr/add | solution.py:143
  128.3 2.2 %fusion.7 = bf16[8,3712]{1,0:T(8,128)(2,1)} fusion(bf16[29,128,128]{2,1,0:T(8,128)(2,1)} %gather_fusion, f32[32,3712]{1,0:T(8,128)S(1)} %get-tuple-element.182, s32[]{:T(128)S(6)} %select_n.144, f32[8,128]{1,0:T(8,128)S(1)} %tile.112), kind=kOutput, calls=%fused_computation.26 | convolution fusion | flops 7691264 | bytes 1132548 | tf_op jit(solution)/shard_map/acx,cxy->acy/dot_general | solution.py:156
  (95 shorter events, 1.5 us)
Async XLA Ops:
  6.5 33.8 %copy-start = (bf16[896,896]{1,0:T(8,128)(2,1)S(1)}, bf16[896,896]{1,0:T(8,128)(2,1)}, u32[]{:S(2)}) copy-start(bf16[896,896]{1,0:T(8,128)(2,1)} %param.25) | copy-start | bytes 4816900
  6.5 114.5 %all-gather.7.cloned.1.call-start = ((), (), s32[]{:S(2)}) async-start(), calls=%async_computation | async-start | bytes 2375680 | tf_op jit(solution)/shard_map/all_gather | solution.py:44
  6.5 3.7 %collective-permute-start = (bf16[1,8,3712]{2,1,0:T(8,128)(2,1)}, bf16[1,8,3712]{2,1,0:T(8,128)(2,1)S(1)}, u32[]{:S(2)}, u32[]{:S(2)}) collective-permute-start(bf16[1,8,3712]{2,1,0:T(8,128)(2,1)} %bitcast.124), channel_id=1, source_target_pairs={{0,4},{4,0},{8,12},{12,8},{16,20},{20,16},{24,28},{28,24},{1,5},{5... | collective-permute-start | bytes 178184 | tf_op jit(solution)/shard_map/ppermute | solution.py:26
  11.1 6.5 %collective-permute-start.1 = (bf16[2,8,3712]{2,1,0:T(8,128)(2,1)S(1)}, bf16[2,8,3712]{2,1,0:T(8,128)(2,1)S(1)}, u32[]{:S(2)}, u32[]{:S(2)}) collective-permute-start(bf16[2,8,3712]{2,1,0:T(8,128)(2,1)S(1)} %pad_maximum_fusion.1), channel_id=1, source_target_pairs={{0,8},{4,12},{8,0},{12,4},{16,24},{20,28},{24,16},{28,20},{1,9},{5... | collective-permute-start | bytes 356360 | tf_op jit(solution)/shard_map/ppermute | solution.py:26
  17.7 3.5 %copy-start.18 = (bf16[2,8,3712]{2,1,0:T(8,128)(2,1)}, bf16[2,8,3712]{2,1,0:T(8,128)(2,1)S(1)}, u32[]{:S(2)}) copy-start(bf16[2,8,3712]{2,1,0:T(8,128)(2,1)S(1)} %get-tuple-element.204) | copy-start | bytes 356356
  17.7 3.5 %copy-start.20 = (bf16[2,8,3712]{2,1,0:T(8,128)(2,1)}, bf16[2,8,3712]{2,1,0:T(8,128)(2,1)S(1)}, u32[]{:S(2)}) copy-start(bf16[2,8,3712]{2,1,0:T(8,128)(2,1)S(1)} %get-tuple-element.205) | copy-start | bytes 356356
  18.5 13.8 %collective-permute-start.2 = (bf16[4,8,3712]{2,1,0:T(8,128)(2,1)}, bf16[4,8,3712]{2,1,0:T(8,128)(2,1)}, u32[]{:S(2)}, u32[]{:S(2)}) collective-permute-start(bf16[4,8,3712]{2,1,0:T(8,128)(2,1)} %pad_maximum_fusion), channel_id=1, source_target_pairs={{0,16},{4,20},{8,24},{12,28},{16,0},{20,4},{24,8},{28,12},{1,17},{... | collective-permute-start | bytes 712712 | tf_op jit(solution)/shard_map/ppermute | solution.py:26
  25.3 1.6 %copy-start.12 = (f32[512,128]{0,1:T(8,128)S(1)}, f32[512,128]{0,1:T(8,128)}, u32[]{:S(2)}) copy-start(f32[512,128]{0,1:T(8,128)} %fusion.13) | copy-start | bytes 786436
  27.1 5.2 %copy-start.19 = (bf16[2,8,3712]{2,1,0:T(8,128)(2,1)S(1)}, bf16[2,8,3712]{2,1,0:T(8,128)(2,1)}, u32[]{:S(2)}) copy-start(bf16[2,8,3712]{2,1,0:T(8,128)(2,1)} %copy-done.18) | copy-start | bytes 356356
  27.1 5.2 %copy-start.21 = (bf16[2,8,3712]{2,1,0:T(8,128)(2,1)S(1)}, bf16[2,8,3712]{2,1,0:T(8,128)(2,1)}, u32[]{:S(2)}) copy-start(bf16[2,8,3712]{2,1,0:T(8,128)(2,1)} %copy-done.20) | copy-start | bytes 356356
  37.6 2.7 %copy-start.7 = (f32[512,896]{1,0:T(8,128)S(1)}, f32[512,896]{1,0:T(8,128)}, u32[]{:S(2)}) copy-start(f32[512,896]{1,0:T(8,128)} %copy.53) | copy-start | bytes 5505028
  40.3 2.5 %copy-start.4 = (bf16[512,3712]{1,0:T(8,128)(2,1)}, bf16[512,3712]{1,0:T(8,128)(2,1)S(1)}, u32[]{:S(2)}) copy-start(bf16[512,3712]{1,0:T(8,128)(2,1)S(1)} %broadcast_select_fusion) | copy-start | bytes 11403268
  40.4 2.5 %copy-start.23 = (f32[128]{0:T(128)S(1)}, f32[128]{0:T(128)}, u32[]{:S(2)}) copy-start(f32[128]{0:T(128)} %param.30) | copy-start | bytes 1540
  40.4 4.4 %copy-start.22 = (f32[1,8,512]{2,1,0:T(8,128)S(1)}, f32[1,8,512]{2,1,0:T(8,128)}, u32[]{:S(2)}) copy-start(f32[1,8,512]{2,1,0:T(8,128)} %param.23) | copy-start | bytes 49156
  40.4 4.8 %copy-start.1 = (f32[512,768]{1,0:T(8,128)S(1)}, f32[512,768]{1,0:T(8,128)}, u32[]{:S(2)}) copy-start(f32[512,768]{1,0:T(8,128)} %copy.57) | copy-start | bytes 4718596
  45.2 3.7 %copy-start.5 = (bf16[512,3712]{1,0:T(8,128)(2,1)S(1)}, bf16[512,3712]{1,0:T(8,128)(2,1)}, u32[]{:S(2)}) copy-start(bf16[512,3712]{1,0:T(8,128)(2,1)} %copy-done.4) | copy-start | bytes 11403268
  45.2 3.7 %copy-start.11 = (bf16[768,768]{1,0:T(8,128)(2,1)S(1)}, bf16[768,768]{1,0:T(8,128)(2,1)}, u32[]{:S(2)}) copy-start(bf16[768,768]{1,0:T(8,128)(2,1)} %param.27) | copy-start | bytes 3538948
  48.9 2.0 %copy-start.2 = (f32[512,640]{1,0:T(8,128)S(1)}, f32[512,640]{1,0:T(8,128)}, u32[]{:S(2)}) copy-start(f32[512,640]{1,0:T(8,128)} %copy.60) | copy-start | bytes 3932164
  48.9 2.0 %copy-start.16 = (bf16[640,640]{1,0:T(8,128)(2,1)S(1)}, bf16[640,640]{1,0:T(8,128)(2,1)}, u32[]{:S(2)}) copy-start(bf16[640,640]{1,0:T(8,128)(2,1)} %param.28) | copy-start | bytes 2457604
  50.9 1.9 %copy-start.14 = (bf16[640,640]{1,0:T(8,128)(2,1)S(1)}, bf16[640,640]{1,0:T(8,128)(2,1)}, u32[]{:S(2)}) copy-start(bf16[640,640]{1,0:T(8,128)(2,1)} %param.29) | copy-start | bytes 2457604
  67.4 4.2 %copy-start.6 = (bf16[512,3712]{1,0:T(8,128)(2,1)S(1)}, bf16[512,3712]{1,0:T(8,128)(2,1)}, u32[]{:S(2)}) copy-start(bf16[512,3712]{1,0:T(8,128)(2,1)} %copy-done.4) | copy-start | bytes 11403268
  67.4 4.2 %copy-start.8 = (f32[512,768]{1,0:T(8,128)S(1)}, f32[512,768]{1,0:T(8,128)}, u32[]{:S(2)}) copy-start(f32[512,768]{1,0:T(8,128)} %fusion.31) | copy-start | bytes 4718596
  67.4 7.6 %copy-start.10 = (f32[512,640]{1,0:T(8,128)S(1)}, f32[512,640]{1,0:T(8,128)}, u32[]{:S(2)}) copy-start(f32[512,640]{1,0:T(8,128)} %fusion.30) | copy-start | bytes 3932164
  71.6 3.4 %copy-start.3 = (f32[512,640]{1,0:T(8,128)S(1)}, f32[512,640]{1,0:T(8,128)}, u32[]{:S(2)}) copy-start(f32[512,640]{1,0:T(8,128)} %copy.60) | copy-start | bytes 3932164
  71.6 3.4 %copy-start.15 = (bf16[640,640]{1,0:T(8,128)(2,1)S(1)}, bf16[640,640]{1,0:T(8,128)(2,1)}, u32[]{:S(2)}) copy-start(bf16[640,640]{1,0:T(8,128)(2,1)} %param.29) | copy-start | bytes 2457604
  71.6 5.4 %copy-start.17 = (bf16[640,640]{1,0:T(8,128)(2,1)S(1)}, bf16[640,640]{1,0:T(8,128)(2,1)}, u32[]{:S(2)}) copy-start(bf16[640,640]{1,0:T(8,128)(2,1)} %param.28) | copy-start | bytes 2457604
  71.6 7.2 %slice-start = ((s8[7602176]{0:T(1024)(128)(4,1)}), s8[4194304]{0:T(1024)(128)(4,1)S(1)}, s32[]{:S(2)}) async-start(s8[7602176]{0:T(1024)(128)(4,1)} %bitcast.113), calls=%async_computation.1 | async-start | bytes 8388608
  75.0 2.0 %copy-start.9 = (f32[512,640]{1,0:T(8,128)S(1)}, f32[512,640]{1,0:T(8,128)}, u32[]{:S(2)}) copy-start(f32[512,640]{1,0:T(8,128)} %fusion.29) | copy-start | bytes 3932164
  75.0 3.8 %slice-start.1 = ((s8[7602176]{0:T(1024)(128)(4,1)}), s8[3407872]{0:T(1024)(128)(4,1)S(1)}, s32[]{:S(2)}) async-start(s8[7602176]{0:T(1024)(128)(4,1)} %bitcast.113), calls=%async_computation.2 | async-start | bytes 6815744
  78.9 7.3 %copy-start.24 = (s32[29]{0:T(128)S(1)}, s32[29]{0:T(128)}, u32[]{:S(2)}) copy-start(s32[29]{0:T(128)} %constant.138) | copy-start | bytes 352
  78.9 7.3 %copy-start.13 = (bf16[7,128,128]{2,1,0:T(8,128)(2,1)S(1)}, bf16[7,128,128]{2,1,0:T(8,128)(2,1)}, u32[]{:S(2)}) copy-start(bf16[7,128,128]{2,1,0:T(8,128)(2,1)} %param.31) | copy-start | bytes 688132
Sparse Core Ops, SparseCore 0:
  86.3 34.7 all-gather.6
